TPU v7x, 128 devices: a whole 4x4x4 slice. The times are simulated.
128 devices in a mesh: dp: 64 (over y, z, x_lo, core), tensor: 2 (over x_hi).
Axes of the slice: x: 4 (x_hi: 2, x_lo: 2; x = x_hi * 2 + x_lo), y: 4, z: 4, core: 2. Of those that a mesh axis runs over, the one named last changes fastest.
Arguments:
- expert_act: bfloat16 [65536, 2880], P(('dp', 'tensor')), may hold values from -6 to 6
- grad_out: bfloat16 [131072, 1440], P(('dp', 'tensor')), may hold values from -6 to 6
- slot_token: int32 [65536], P(('dp', 'tensor')), may hold values from 0 to 1023, as said below
- slot_prob: float32 [65536], P(('dp', 'tensor')), may hold values from 0.2 to 1
- live_count: int32 [128], P(('dp', 'tensor')), may hold values from 128 to 512, as said below
Outputs:
- weight_grad: float32 [2880, 1440], P('dp', 'tensor')
Inputs may be any that keep to these rules, and one draw needn't show every extreme that they name: `slot_token`: each device's 512 entries are distinct token indices of that device. `live_count`: each entry is 512 // j for some j of 1 to 4.
All inputs are finite; a program needn't handle non-finite values.
Results may differ from a plain program's by a relative error of at most 0.0029.
Values may be sent and summed in bfloat16 or wider, within the bound.
A program may use at most 128 MiB of HBM per device.

v0:
```python
import math

import jax
import jax.numpy as jnp
from jax import lax
from jax.sharding import Mesh
from jax.sharding import PartitionSpec as P

DP = ("dp_0", "dp_1", "dp_2", "dp_3")
DP_TENSOR = ("dp_0", "dp_1", "dp_2", "dp_3", "tensor")


def in_blocks(shard, dim, length):
    before, after = (shard.shape[:dim], shard.shape[dim + 1 :])
    return jnp.moveaxis(shard.reshape(*before, length, -1, *after), dim, 0)


def summed_rows(shard, chips, core, dim):
    sizes = (lax.axis_size(chips), lax.axis_size(core))
    pieces = in_blocks(shard, dim, sizes[0] * sizes[1])
    inside = pieces.shape[1:]
    pieces = pieces.reshape(*sizes, *inside).swapaxes(0, 1).reshape(-1, *inside)
    pieces = lax.psum_scatter(pieces, core, scatter_dimension=0, tiled=True)
    return lax.psum_scatter(pieces, chips, scatter_dimension=0, tiled=True)[0]


def sent_and_summed(shard, axis, dim):
    length = lax.axis_size(axis)
    pieces = lax.all_to_all(in_blocks(shard, dim, length), axis, 0, 0, tiled=True)
    return jnp.sum(pieces, axis=0)


def contract(left, right):
    return lax.dot_general(
        left, right, (((0,), (0,)), ((), ())), preferred_element_type=jnp.float32
    )


def shards(expert_act, grad_out, slot_token, slot_prob, live_count):
    slot_count = expert_act.shape[0]
    devices = lax.axis_size(DP) * lax.axis_size("tensor")
    scaling = 1.0 / math.sqrt(slot_count * devices)
    position = jnp.arange(slot_count, dtype=jnp.int32)
    live_mask = position < live_count[0]
    weighting = jnp.where(live_mask, slot_prob, jnp.zeros_like(slot_prob))
    picked = jnp.take(grad_out, slot_token, axis=0).astype(jnp.float32)
    weighted = (picked * weighting[:, None]).astype(jnp.bfloat16)
    partial_value = summed_rows(contract(expert_act, weighted), ("dp_0", "dp_1", "dp_2"), "dp_3", 0)
    gradient = sent_and_summed(partial_value, "tensor", 1)
    return gradient * scaling


def solution(mesh):
    finer = Mesh(
        mesh.devices.reshape(4, 4, 2, 2, mesh.shape["tensor"]),
        ("dp_0", "dp_1", "dp_2", "dp_3", "tensor"),
    )
    return jax.shard_map(
        shards,
        mesh=finer,
        in_specs=(P(DP_TENSOR, None), P(DP_TENSOR, None), P(DP_TENSOR), P(DP_TENSOR), P(DP_TENSOR)),
        out_specs=P(DP, "tensor"),
        check_vma=False,
    )
```

profile of v0, /device:TPU:0, one launch (start us, length us, event | category | flops | bytes accessed | tf_op | source)
XLA Modules:
  0.0 539.6 jit_solution(508220922620338518)
XLA Ops:
  6.5 0.0 copy-start
  6.5 0.0 reduce-scatter.3.cloned.1.call-start
  6.5 0.8 compare_select_fusion
  7.4 0.8 compare_and_fusion
  8.1 4.6 copy.10
  13.4 0.0 copy-start.2
  13.4 6.7 %gather_fusion = bf16[512,1440]{1,0:T(8,128)(2,1)} fusion(bf16[1024,1440]{1,0:T(8,128)(2,1)} %copy.10, s32[1024]{0:T(1024)S(1)} %pad_clamp_fusion), kind=kCustom, calls=%fused_computation | custom fusion | bytes 2951168 | tf_op jit(solution)/shard_map/jit(_take)/gather | solution.py:46
  20.1 10.5 %convolution_bitcast_fusion = f32[2880,1440]{0,1:T(8,128)} fusion(bf16[512,2880]{0,1:T(8,128)(2,1)S(1)} %copy-done, f32[512]{0:T(512)S(1)} %fusion.4, bf16[512,1440]{1,0:T(8,128)(2,1)} %gather_fusion, pred[512]{0:T(512)(128)(4,1)S(1)} %compare_and_fusion), kind=kOutput, calls=%fused_computation.1 | convolution fusion | flops 4249681920 | bytes 21015040 | tf_op jit(solution)/shard_map/dot_general | solution.py:34
  30.6 18.1 %copy.11 = f32[2880,1440]{1,0:T(8,128)} copy(f32[2880,1440]{0,1:T(8,128)} %convolution_bitcast_fusion) | data formatting | bytes 33177600 | tf_op jit(solution)/shard_map/dot_general | solution.py:34
  48.7 14.9 %reshape_reshape.3 = f32[32,2,45,1440]{3,2,1,0:T(8,128)} reshape(f32[2880,1440]{1,0:T(8,128)} %copy.11) | data formatting | bytes 33177600 | tf_op jit(solution)/shard_map/reshape;reshape | solution.py:22
  63.6 18.7 %copy.12 = f32[2,32,45,1440]{3,1,0,2:T(8,128)} copy(f32[2,32,45,1440]{3,2,0,1:T(8,128)} %bitcast.9) | data formatting | bytes 33177600 | tf_op jit(solution)/shard_map/transpose | solution.py:22
  82.4 0.0 reduce-scatter.3.cloned.1.call-update
  82.4 0.0 all-reduce.3.cloned.1.call-start
  82.4 30.9 %reduce-scatter.3.cloned.1.call-done = f32[32,45,1440]{2,0,1:T(8,128)} async-done(((f32[64,45,1440]{2,0,1:T(8,128)}), f32[32,45,1440]{2,0,1:T(8,128)}) %reduce-scatter.3.cloned.1.call-update) | async-done | bytes 8294416 | tf_op jit(solution)/shard_map/reduce_scatter | solution.py:23
  113.3 0.0 all-reduce.3.cloned.1.call-update
  113.4 0.0 copy-start.1
  113.4 0.6 copy-done.3
  114.0 0.6 dynamic-slice
  114.6 403.6 %all-reduce.3.cloned.1.call-done = f32[32,45,1440]{2,0,1:T(8,128)} async-done(((f32[32,45,1440]{2,0,1:T(8,128)}), f32[32,45,1440]{2,0,1:T(8,128)}) %all-reduce.3.cloned.1.call-update) | async-done | bytes 8294416
  518.1 3.0 dynamic-slice_reduce_fusion
  521.2 0.3 reshape_squeeze.3
  521.5 10.6 %all_to_all.5 = f32[2,45,720]{2,1,0:T(8,128)S(1)} all-to-all(f32[2,45,720]{2,1,0:T(8,128)S(1)} %copy.13), channel_id=1, replica_groups=mesh['dp_0'=4,'dp_1'=4,'dp_2'=2,'dp_3'=2,'tensor'=2] {'tensor'}, dimensions={0} | all-to-all | bytes 518400 | tf_op jit(solution)/shard_map/all_to_all | solution.py:29
  532.1 0.7 broadcast_multiply_fusion
  532.8 0.0 copy-done.1
  (7 shorter events, 0.1 us)
Async XLA Ops:
  6.5 13.6 %copy-start = (bf16[512,2880]{0,1:T(8,128)(2,1)S(1)}, bf16[512,2880]{0,1:T(8,128)(2,1)}, u32[]{:S(2)}) copy-start(bf16[512,2880]{0,1:T(8,128)(2,1)} %param.5) | copy-start | bytes 8847364
  6.5 106.8 %reduce-scatter.3.cloned.1.call-start = ((), (), s32[]{:S(2)}) async-start(), calls=%async_computation.2 | async-start | bytes 26542080 | tf_op jit(solution)/shard_map/reduce_scatter | solution.py:23
  13.4 6.7 %copy-start.2 = (f32[512]{0:T(512)S(1)}, f32[512]{0:T(512)}, u32[]{:S(2)}) copy-start(f32[512]{0:T(512)} %param.8) | copy-start | bytes 6148
  82.4 435.8 %all-reduce.3.cloned.1.call-start = ((), (), s32[]{:S(2)}) async-start(), calls=%async_computation.3 | async-start | bytes 17694720
  113.3 0.7 copy-start.3
  113.4 419.4 %copy-start.1 = (bf16[512,2880]{0,1:T(8,128)(2,1)S(1)}, bf16[512,2880]{0,1:T(8,128)(2,1)}, u32[]{:S(2)}) copy-start(bf16[512,2880]{0,1:T(8,128)(2,1)} %param.5) | copy-start | bytes 8847364
Sparse Core Ops, SparseCore 0:
  82.5 30.7 reduce-scatter.2
  115.9 402.2 all-reduce.2
where the time goes:
time: 541 us; the launch traced here: 540 us
  waiting for transfers between devices  434 us (80%)
  local copies, waits for them, and re-layouts  67.6 us (12%)
  between operations  14.1 us (3%)
  blocking collectives  10.6 us (2%)
  matrix products  10.5 us (2%)
    unnamed x3, waiting for transfers between devices  404 us
    reduce_scatter x1, waiting for transfers between devices, summed_rows(): pieces = lax.psum_scatter(pieces, core, scatter_dimension=0, tiled=True)  30.9 us
    transpose x1, local copies, waits for them, and re-layouts, summed_rows(): pieces = pieces.reshape(*sizes, *inside).swapaxes(0, 1).reshape(-1, *inside)  18.7 us
    dot_general x1, local copies, waits for them, and re-layouts, contract(): lax.dot_general(left, right, (((0,), (0,)), ((), ())), preferred_element_...  18.1 us
    another operation x1, local copies, waits for them, and re-layouts, summed_rows(): pieces = pieces.reshape(*sizes, *inside).swapaxes(0, 1).reshape(-1, *inside)  14.9 us
  transfers between devices with their start and end apart: 2, of which 2 were waited for; matrix products, arithmetic and copies ran while one was open for 0% of the time, Pallas kernels for 0%

commit v1 on v0

v1 whole, which is shorter than its diff:
```python
import functools
import math

import jax
import jax.numpy as jnp
from jax import lax
from jax.experimental import pallas as pl
from jax.experimental.pallas import tpu as pltpu
from jax.sharding import PartitionSpec as P

MESH = pl.DeviceIdType.MESH
F32, BF16 = jnp.float32, jnp.bfloat16
ROWS, PAD = 45, 48
WIDTHS = (256, 256, 208)
STARTS = (0, 256, 512)
HALF = 720
A_MSG, W_MSG, S1, S2, S3, N_MSG = 0, 1, 4, 22, 31, 40


def nt(left, right):
    return lax.dot_general(left, right, (((1,), (1,)), ((), ())), preferred_element_type=F32)


def kernel(
    scaling, tok_ref, prob_ref, live_ref, a_hbm, g_hbm, out_ref,
    a_v, g_v, hot, ap, ao, wp, wo, s1, r1, keep, acc, s2, r2, s3, r3,
    load_sem, send_sem, recv_sem,
):
    dp, x_hi = lax.axis_index("dp"), lax.axis_index("tensor")
    core = lax.rem(dp, 2)
    x_lo = lax.rem(lax.div(dp, 2), 2)
    z = lax.rem(lax.div(dp, 4), 4)
    y = lax.div(dp, 16)
    x = x_hi * 2 + x_lo

    def at(cx, cy, cz, cc):
        return (((cy * 4 + cz) * 2 + lax.rem(cx, 2)) * 2 + cc, lax.div(cx, 2))

    def moved(dim, by):
        place = {"x": x, "y": y, "z": z}
        place[dim] = lax.rem(place[dim] + by, 4)
        return at(place["x"], place["y"], place["z"], core)

    partner = at(x, y, z, 1 - core)
    here = {"x": x, "y": y, "z": z}
    orders = ("yzx", "zxy", "xyz")

    load_g = pltpu.make_async_copy(g_hbm, g_v, load_sem.at[0])
    load_a = pltpu.make_async_copy(a_hbm, a_v, load_sem.at[1])
    load_a.start()
    load_g.start()

    barrier = pltpu.get_barrier_semaphore()
    peers = [partner] + [moved(d, by) for d in "xyz" for by in (1, 2, 3)]
    for peer in peers:
        pl.semaphore_signal(barrier, inc=1, device_id=peer, device_id_type=MESH)

    sent = []

    def send(src, dst, index, device):
        copy = pltpu.make_async_remote_copy(
            src_ref=src, dst_ref=dst, send_sem=send_sem.at[index], recv_sem=recv_sem.at[index],
            device_id=device, device_id_type=MESH,
        )
        copy.start()
        sent.append(copy)
        return copy

    tokens, slots = hot.shape
    for start in range(0, tokens, 256):
        rows = lax.broadcasted_iota(jnp.int32, (256, slots), 0) + start
        hot[start : start + 256, :] = (rows == tok_ref[...]).astype(F32).astype(BF16)
    position = lax.broadcasted_iota(jnp.int32, (1, slots), 1)
    weighting = jnp.where(position < live_ref[0], prob_ref[...], jnp.zeros((1, slots), F32))

    load_a.wait()
    for parity in range(2):
        for q in range(32):
            first = ROWS * (2 * q + parity)
            base = first // 16 * 16
            stop = min(base + 64, a_v.shape[0])
            block = a_v[base:stop, :].astype(F32)[first - base : first - base + ROWS]
            block = jnp.concatenate([block, jnp.zeros((PAD - ROWS, slots), F32)], axis=0)
            ap[parity, q // 8, q // 2 % 4, q % 2] = block.astype(BF16)

    pl.semaphore_wait(barrier, len(peers))
    a_copy = send(ap.at[1 - core], ao, A_MSG, partner)

    load_g.wait()
    w_copies = []
    for k in range(3):
        width = WIDTHS[k]
        for half in range(2):
            first = half * HALF + STARTS[k]
            picked = jnp.dot(g_v[first : first + width, :], hot[...], preferred_element_type=F32)
            wp[k, half, :width, :] = (picked * weighting).astype(BF16)
            if width < 256:
                wp[k, half, width:, :] = jnp.zeros((256 - width, slots), BF16)
        w_copies.append(send(wp.at[k], wo.at[k], W_MSG + k, partner))

    a_copy.wait_recv()
    for copy in w_copies:
        copy.wait_recv()

    def unit(k, place, half):
        if k == 0:
            own, other, right = ap[core, place], ao[place], (k, half)
        elif k == 1:
            own, other, right = ap[core, :, place], ao[:, place], (k, half)
        else:
            low = lax.rem(place, 2)
            own = ap[core, 2 * half : 2 * half + 2, :, low]
            other = ao[2 * half : 2 * half + 2, :, low]
            right = (k, lax.div(place, 2))
        own, other = own.reshape(8 * PAD, slots), other.reshape(8 * PAD, slots)
        return (nt(own, wp[right]) + nt(other, wo[right])).reshape(8, PAD, 256)

    def first_stage(k, message, device):
        index = k * 6 + message
        return send(s1.at[k, message], r1.at[k, message], S1 + index, device)

    firsts = [[None] * 6 for _ in range(3)]
    for k in range(3):
        dim = orders[k][0]
        far = lax.rem(here[dim] + 2, 4)
        for half in range(2):
            s1[k, half] = unit(k, far, half).astype(BF16)
            firsts[k][half] = first_stage(k, half, moved(dim, 1 if half == 0 else 3))
    for k in range(3):
        dim = orders[k][0]
        up, down = lax.rem(here[dim] + 1, 4), lax.rem(here[dim] + 3, 4)
        s1[k, 2] = unit(k, up, 1).astype(BF16)
        firsts[k][2] = first_stage(k, 2, moved(dim, 1))
        s1[k, 3] = unit(k, down, 0).astype(BF16)
        firsts[k][3] = first_stage(k, 3, moved(dim, 3))
    for k in range(3):
        dim = orders[k][0]
        up, down = lax.rem(here[dim] + 1, 4), lax.rem(here[dim] + 3, 4)
        keep[k, 0] = unit(k, up, 0)
        keep[k, 1] = unit(k, down, 1)
    for k in range(3):
        for half in range(2):
            acc[k, half] = unit(k, here[orders[k][0]], half)
    for k in range(3):
        dim = orders[k][0]
        for half in range(2):
            firsts[k][half].wait_recv()
            s1[k, 4 + half] = (keep[k, half] + r1[k, half].astype(F32)).astype(BF16)
            firsts[k][4 + half] = first_stage(k, 4 + half, moved(dim, 1 if half == 0 else 3))
    for k in range(3):
        for message in (2, 3):
            firsts[k][message].wait_recv()
        acc[k, 0] = acc[k, 0] + r1[k, 3].astype(F32)
        acc[k, 1] = acc[k, 1] + r1[k, 2].astype(F32)

    seconds = [[None] * 3 for _ in range(3)]
    for k in range(3):
        dim = orders[k][1]
        for half in range(2):
            firsts[k][4 + half].wait_recv()
            acc[k, half] = acc[k, half] + r1[k, 4 + half].astype(F32)

    def stage_two(k, place):
        if k == 0:
            return acc[0, :, pl.ds(place * 2, 2)].reshape(4, PAD, 256)
        if k == 1:
            hi, lo = lax.div(place, 2), lax.rem(place, 2)
            return jnp.stack([acc[1, hi, 2 * cy + lo] for cy in range(4)])
        hi, lo = lax.div(place, 2), lax.rem(place, 2)
        return acc[2, hi, pl.ds(lo * 4, 4)]

    for k in range(3):
        dim = orders[k][1]
        for i, by in enumerate((2, 1, 3)):
            s2[k, i] = stage_two(k, lax.rem(here[dim] + by, 4)).astype(BF16)
            seconds[k][i] = send(s2.at[k, i], r2.at[k, i], S2 + 3 * k + i, moved(dim, by))
    for k in range(3):
        total = stage_two(k, here[orders[k][1]])
        for i in range(3):
            seconds[k][i].wait_recv()
            total = total + r2[k, i].astype(F32)
        keep[k, 0, 0:4] = total

    thirds = [[None] * 3 for _ in range(3)]
    for k in range(3):
        dim = orders[k][2]
        for i, by in enumerate((2, 1, 3)):
            s3[k, i] = keep[k, 0, lax.rem(here[dim] + by, 4)].astype(BF16)
            thirds[k][i] = send(s3.at[k, i], r3.at[k, i], S3 + 3 * k + i, moved(dim, by))
    for k in range(3):
        total = keep[k, 0, here[orders[k][2]]]
        for i in range(3):
            thirds[k][i].wait_recv()
            total = total + r3[k, i].astype(F32)
        out_ref[:, STARTS[k] : STARTS[k] + WIDTHS[k]] = (total * scaling)[:ROWS, : WIDTHS[k]]
    for copy in sent:
        copy.wait_send()


def solution(mesh):
    devices = mesh.shape["dp"] * mesh.shape["tensor"]

    def step(expert_act, grad_out, slot_token, slot_prob, live_count):
        slots, hidden = expert_act.shape
        tokens, features = grad_out.shape
        scaling = 1.0 / math.sqrt(slots * devices)
        blocks = (4, 4, 2, PAD)
        vmem = lambda *shape: pltpu.VMEM(shape, BF16)
        vmem32 = lambda *shape: pltpu.VMEM(shape, F32)
        return pl.pallas_call(
            functools.partial(kernel, scaling),
            out_shape=jax.ShapeDtypeStruct((ROWS, HALF), F32),
            in_specs=[
                pl.BlockSpec(memory_space=pltpu.VMEM),
                pl.BlockSpec(memory_space=pltpu.VMEM),
                pl.BlockSpec(memory_space=pltpu.SMEM),
                pl.BlockSpec(memory_space=pl.ANY),
                pl.BlockSpec(memory_space=pl.ANY),
            ],
            out_specs=pl.BlockSpec(memory_space=pltpu.VMEM),
            scratch_shapes=[
                vmem(hidden, slots), vmem(features, tokens), vmem(tokens, slots),
                vmem(2, *blocks, slots), vmem(*blocks, slots),
                vmem(3, 2, 256, slots), vmem(3, 2, 256, slots),
                vmem(3, 6, 8, PAD, 256), vmem(3, 6, 8, PAD, 256),
                vmem32(3, 2, 8, PAD, 256), vmem32(3, 2, 8, PAD, 256),
                vmem(3, 3, 4, PAD, 256), vmem(3, 3, 4, PAD, 256),
                vmem(3, 3, PAD, 256), vmem(3, 3, PAD, 256),
                pltpu.SemaphoreType.DMA((2,)),
                pltpu.SemaphoreType.DMA((N_MSG,)),
                pltpu.SemaphoreType.DMA((N_MSG,)),
            ],
            compiler_params=pltpu.CompilerParams(collective_id=0, has_side_effects=True),
        )(slot_token.reshape(1, slots), slot_prob.reshape(1, slots), live_count, expert_act.T, grad_out.T)

    both = ("dp", "tensor")
    return jax.shard_map(
        step,
        mesh=mesh,
        in_specs=(P(both, None), P(both, None), P(both), P(both), P(both)),
        out_specs=P("dp", "tensor"),
        check_vma=False,
    )
```

time: 541 us -> 46.6 us (0.09)
  waiting for transfers between devices: 434 us -> 0 us
  local copies, waits for them, and re-layouts: 67.6 us -> 1.58 us
  Pallas kernels: 0 us -> 44.1 us
  between operations: 14.1 us -> 0.66 us
  blocking collectives: 10.6 us -> 0 us
  matrix products: 10.5 us -> 0 us
    unnamed x3 -> x0, waiting for transfers between devices: 404 us -> none
    pallas_call x0 -> x1, Pallas kernels: none -> 44.1 us  [step(): pl.pallas_call(functools.partial(kernel, scaling), out_shape=jax.ShapeDty...]
    reduce_scatter x1 -> x0, waiting for transfers between devices: 30.9 us -> none  [summed_rows(): pieces = lax.psum_scatter(pieces, core, scatter_dimension=0, tiled=True)]
    transpose x2 -> x0, local copies, waits for them, and re-layouts: 18.8 us -> none  [the longest x1 18.7 us: summed_rows(): pieces = pieces.reshape(*sizes, *inside).swapaxes(0, 1).reshape(-1, *inside)]
    dot_general x1 -> x0, local copies, waits for them, and re-layouts: 18.1 us -> none  [contract(): lax.dot_general(left, right, (((0,), (0,)), ((), ())), preferred_element_...]
    another operation x2 -> x0, local copies, waits for them, and re-layouts: 15.2 us -> none  [the longest x1 14.9 us: summed_rows(): pieces = pieces.reshape(*sizes, *inside).swapaxes(0, 1).reshape(-1, *inside)]
    all_to_all x1 -> x0, blocking collectives: 10.6 us -> none  [sent_and_summed(): lax.all_to_all(in_blocks(shard, dim, length), axis, 0, 0, tiled=True)]
    dot_general x1 -> x0, matrix products: 10.5 us -> none  [contract(): lax.dot_general(left, right, (((0,), (0,)), ((), ())), preferred_element_...]
  transfers between devices with their start and end apart: 2 -> 0, of which waited for: 2 -> 0; matrix products, arithmetic and copies ran while one was open for 0% -> 0% of each run, Pallas kernels for 0% -> 0%
where the time goes in v1:
time: 46.6 us; the launch traced here: 46.3 us
  Pallas kernels  44.1 us (95%)
  local copies, waits for them, and re-layouts  1.58 us (3%)
  between operations  0.66 us (1%)
    pallas_call x1, Pallas kernels, step(): pl.pallas_call(functools.partial(kernel, scaling), out_shape=jax.ShapeDty...  44.1 us
    unnamed x1, local copies, waits for them, and re-layouts  1.58 us

profile of v1, /device:TPU:0, one launch (start us, length us, event | category | flops | bytes accessed | tf_op | source)
XLA Modules:
  0.0 46.3 jit_solution(3082737869577897987)
XLA Ops:
  0.7 44.1 %shard_map.55 = f32[45,720]{1,0:T(8,128)} custom-call(s32[1,512]{1,0:T(1,128)} %bitcast.6, f32[1,512]{1,0:T(1,128)} %bitcast.7, s32[1]{0:T(128)S(6)} %copy.7.live_ref, bf16[2880,512]{1,0:T(8,128)(2,1)} %bitcast.4, bf16[1440,1024]{1,0:T(8,128)(2,1)} %bitcast.5), custom_call_target="tpu_custom_call" | custom-call | tf_op jit(solution)/shard_map/pallas_call | solution.py:210
  44.8 1.6 %copy.8 = f32[45,720]{1,0:T(8,128)} copy(f32[45,720]{1,0:T(8,128)} %shard_map.55) | data formatting | bytes 259200

commit v2 on v1

v2 whole, which is shorter than its diff:
```python
import math

import jax
import jax.numpy as jnp
from jax import lax
from jax.experimental import pallas as pl
from jax.experimental.pallas import tpu as pltpu
from jax.sharding import PartitionSpec as P

MESH = pl.DeviceIdType.MESH
F32, BF16 = jnp.float32, jnp.bfloat16
ROWS, PAD = 45, 48
WIDTHS = (256, 256, 208)
STARTS = (0, 256, 512)
HALF = 720
VMEM_LIMIT = 55000000
LANES = 128
A_MSG, W_MSG, S1, S2, S3, N_MSG = 0, 4, 7, 43, 61, 79


def nt(left, right):
    return lax.dot_general(left, right, (((1,), (1,)), ((), ())), preferred_element_type=F32)


def kernel(
    live_ref, tok_hbm, prob_hbm, a_hbm, g_hbm, out_ref,
    tok_ref, prob_ref, a_v, g_v, hot, ap, ao, wp, wo, s1, r1, keep, acc, s2, r2, s3, r3,
    load_sem, send_sem, recv_sem,
):
    dp, x_hi = lax.axis_index("dp"), lax.axis_index("tensor")
    core = lax.rem(dp, 2)
    x_lo = lax.rem(lax.div(dp, 2), 2)
    z = lax.rem(lax.div(dp, 4), 4)
    y = lax.div(dp, 16)
    x = x_hi * 2 + x_lo

    def at(cx, cy, cz, cc):
        return (((cy * 4 + cz) * 2 + lax.rem(cx, 2)) * 2 + cc, lax.div(cx, 2))

    def moved(dim, by):
        place = {"x": x, "y": y, "z": z}
        place[dim] = lax.rem(place[dim] + by, 4)
        return at(place["x"], place["y"], place["z"], core)

    partner = at(x, y, z, 1 - core)
    here = {"x": x, "y": y, "z": z}
    orders = ("yzx", "zxy", "xyz")

    chunk = a_v.shape[0] // 4
    loads = [(a_hbm.at[pl.ds(i * chunk, chunk)], a_v.at[pl.ds(i * chunk, chunk)]) for i in range(4)]
    loads += [(tok_hbm, tok_ref), (prob_hbm, prob_ref)]
    loads += [(g_hbm.at[pl.ds(i * HALF, HALF)], g_v.at[pl.ds(i * HALF, HALF)]) for i in range(2)]
    loads = [pltpu.make_async_copy(src, dst, load_sem.at[i]) for i, (src, dst) in enumerate(loads)]
    for load in loads:
        load.start()

    barrier = pltpu.get_barrier_semaphore()
    peers = [partner] + [moved(d, by) for d in "xyz" for by in (1, 2, 3)]
    for peer in peers:
        pl.semaphore_signal(barrier, inc=1, device_id=peer, device_id_type=MESH)

    sent = []

    def send(src, dst, index, device):
        copy = pltpu.make_async_remote_copy(
            src_ref=src, dst_ref=dst, send_sem=send_sem.at[index], recv_sem=recv_sem.at[index],
            device_id=device, device_id_type=MESH,
        )
        copy.start()
        sent.append(copy)
        return copy

    tokens, slots = hot.shape
    zeros = jnp.zeros((PAD - ROWS, slots), F32)

    def padded(quarter):
        for parity in range(2):
            for q in range(8):
                first = ROWS * (16 * quarter + 2 * q + parity)
                base = first // 8 * 8
                stop = min(base + 56, (quarter + 1) * chunk)
                block = a_v[base:stop, :].astype(F32)[first - base : first - base + ROWS]
                block = jnp.concatenate([block, zeros], axis=0)
                ap[parity, quarter, q // 2, q % 2] = block.astype(BF16)

    a_copies = []
    for quarter in range(4):
        with jax.named_scope(f"pad{quarter}"):
            loads[quarter].wait()
            padded(quarter)
        if quarter == 0:
            with jax.named_scope("barrier"):
                pl.semaphore_wait(barrier, len(peers))
        a_copies.append(send(ap.at[1 - core, quarter], ao.at[quarter], A_MSG + quarter, partner))

    with jax.named_scope("hot"):
        loads[4].wait()
        loads[5].wait()
        for start in range(0, tokens, 256):
            rows = lax.broadcasted_iota(jnp.int32, (256, slots), 0) + start
            hot[start : start + 256, :] = (rows == tok_ref[...]).astype(F32).astype(BF16)
        position = lax.broadcasted_iota(jnp.int32, (1, slots), 1)
        weighting = jnp.where(position < live_ref[0], prob_ref[...], jnp.zeros((1, slots), F32))

    with jax.named_scope("weighted"):
        loads[6].wait()
        loads[7].wait()
        w_copies = []
        for k in range(3):
            width = WIDTHS[k]
            for half in range(2):
                first = half * HALF + STARTS[k]
                picked = jnp.dot(g_v[first : first + width, :], hot[...], preferred_element_type=F32)
                wp[k, half, :width, :] = (picked * weighting).astype(BF16)
                if width < 256:
                    wp[k, half, width:, :] = jnp.zeros((256 - width, slots), BF16)
            w_copies.append(send(wp.at[k], wo.at[k], W_MSG + k, partner))

    with jax.named_scope("swap_a"):
        for copy in a_copies:
            copy.wait_recv()

    def unit(k, place, half):
        if k == 0:
            own, other, right = ap[core, place], ao[place], (k, half)
        elif k == 1:
            own, other, right = ap[core, :, place], ao[:, place], (k, half)
        else:
            low = lax.rem(place, 2)
            own = ap[core, 2 * half : 2 * half + 2, :, low]
            other = ao[2 * half : 2 * half + 2, :, low]
            right = (k, lax.div(place, 2))
        own, other = own.reshape(8 * PAD, slots), other.reshape(8 * PAD, slots)
        return (nt(own, wp[right]) + nt(other, wo[right])).reshape(8, PAD, 256)

    def first_stage(k, part, message, device):
        index = S1 + (k * 2 + part) * 6 + message
        return send(s1.at[k, part, message], r1.at[k, part, message], index, device)

    def both_parts(k, message, value):
        for part in range(2):
            s1[k, part, message] = value[:, :, lanes(part)].astype(BF16)

    def lanes(part):
        return slice(part * LANES, part * LANES + LANES)

    firsts = [[[None] * 6 for _ in range(2)] for _ in range(3)]
    ends = []
    for k in range(3):
        dim = orders[k][0]
        far, up, down = [lax.rem(here[dim] + by, 4) for by in (2, 1, 3)]
        ends.append((dim, far, up, down))
    for k, (dim, far, _, _) in enumerate(ends):
        with jax.named_scope(f"swap_w{k}"):
            w_copies[k].wait_recv()
        with jax.named_scope(f"m1_{k}"):
            for half in range(2):
                both_parts(k, half, unit(k, far, half))
            for part in range(2):
                for half in range(2):
                    firsts[k][part][half] = first_stage(k, part, half, moved(dim, 1 + 2 * half))
    with jax.named_scope("m2"):
        for k, (dim, _, up, down) in enumerate(ends):
            both_parts(k, 2, unit(k, up, 1))
            both_parts(k, 3, unit(k, down, 0))
        for part in range(2):
            for k, (dim, _, up, down) in enumerate(ends):
                firsts[k][part][2] = first_stage(k, part, 2, moved(dim, 1))
                firsts[k][part][3] = first_stage(k, part, 3, moved(dim, 3))
    with jax.named_scope("keep"):
        for k, (dim, _, up, down) in enumerate(ends):
            keep[k, 0] = unit(k, up, 0)
            keep[k, 1] = unit(k, down, 1)
    with jax.named_scope("own"):
        for k, (dim, _, _, _) in enumerate(ends):
            for half in range(2):
                acc[k, half] = unit(k, here[dim], half)
    for part in range(2):
        cols = lanes(part)
        for k, (dim, _, _, _) in enumerate(ends):
            with jax.named_scope(f"m3_{part}{k}"):
                for half in range(2):
                    firsts[k][part][half].wait_recv()
                    s1[k, part, 4 + half] = (keep[k, half, :, :, cols] + r1[k, part, half].astype(F32)).astype(BF16)
                for half in range(2):
                    firsts[k][part][4 + half] = first_stage(k, part, 4 + half, moved(dim, 1 + 2 * half))

    def stage_two(k, place, cols):
        if k == 0:
            return acc[0, :, pl.ds(place * 2, 2), :, cols].reshape(4, PAD, LANES)
        hi, lo = lax.div(place, 2), lax.rem(place, 2)
        if k == 1:
            return jnp.stack([acc[1, hi, 2 * cy + lo, :, cols] for cy in range(4)])
        return acc[2, hi, pl.ds(lo * 4, 4), :, cols]

    seconds, thirds = {}, {}
    for part in range(2):
        cols = lanes(part)
        for k in range(3):
            dim = orders[k][1]
            with jax.named_scope(f"m2_wait_{part}{k}"):
                for message in (2, 3):
                    firsts[k][part][message].wait_recv()
                acc[k, 0, :, :, cols] = acc[k, 0, :, :, cols] + r1[k, part, 3].astype(F32)
                acc[k, 1, :, :, cols] = acc[k, 1, :, :, cols] + r1[k, part, 2].astype(F32)
        for k in range(3):
            dim = orders[k][1]
            with jax.named_scope(f"m3_wait_{part}{k}"):
                for half in range(2):
                    firsts[k][part][4 + half].wait_recv()
                    acc[k, half, :, :, cols] = acc[k, half, :, :, cols] + r1[k, part, 4 + half].astype(F32)
            with jax.named_scope(f"s2_send_{part}{k}"):
                for i, by in enumerate((2, 1, 3)):
                    s2[k, part, i] = stage_two(k, lax.rem(here[dim] + by, 4), cols).astype(BF16)
                for i, by in enumerate((2, 1, 3)):
                    seconds[k, part, i] = send(
                        s2.at[k, part, i], r2.at[k, part, i], S2 + 6 * k + 3 * part + i, moved(dim, by)
                    )
    for part in range(2):
        cols = lanes(part)
        for k in range(3):
            dim = orders[k][2]
            with jax.named_scope(f"s2_wait_{part}{k}"):
                total = stage_two(k, here[orders[k][1]], cols)
                for i in range(3):
                    seconds[k, part, i].wait_recv()
                    total = total + r2[k, part, i].astype(F32)
                keep[k, part, 0:4, :, :LANES] = total
            with jax.named_scope(f"s3_send_{part}{k}"):
                for i, by in enumerate((2, 1, 3)):
                    s3[k, part, i] = keep[k, part, lax.rem(here[dim] + by, 4), :, :LANES].astype(BF16)
                for i, by in enumerate((2, 1, 3)):
                    thirds[k, part, i] = send(
                        s3.at[k, part, i], r3.at[k, part, i], S3 + 6 * k + 3 * part + i, moved(dim, by)
                    )
    for part in range(2):
        for k in range(3):
            with jax.named_scope(f"s3_wait_{part}{k}"):
                total = keep[k, part, here[orders[k][2]], :, :LANES]
                for i in range(3):
                    thirds[k, part, i].wait_recv()
                    total = total + r3[k, part, i].astype(F32)
                first = STARTS[k] + part * LANES
                last = min(first + LANES, STARTS[k] + WIDTHS[k])
                out_ref[:, first:last] = total[:ROWS, : last - first]
    with jax.named_scope('drain'):
        for copy in sent:
            copy.wait_send()


def solution(mesh):
    devices = mesh.shape["dp"] * mesh.shape["tensor"]

    def step(expert_act, grad_out, slot_token, slot_prob, live_count):
        slots, hidden = expert_act.shape
        tokens, features = grad_out.shape
        scaling = 1.0 / math.sqrt(slots * devices)
        blocks = (4, 4, 2, PAD)
        vmem = lambda *shape: pltpu.VMEM(shape, BF16)
        vmem32 = lambda *shape: pltpu.VMEM(shape, F32)
        gradient = pl.pallas_call(
            kernel,
            out_shape=jax.ShapeDtypeStruct((ROWS, HALF), F32),
            in_specs=[
                pl.BlockSpec(memory_space=pltpu.SMEM),
                *[pl.BlockSpec(memory_space=pltpu.HBM)] * 4,
            ],
            out_specs=pl.BlockSpec(memory_space=pltpu.VMEM),
            scratch_shapes=[
                pltpu.VMEM((1, slots), jnp.int32), vmem32(1, slots),
                vmem(hidden, slots), vmem(features, tokens), vmem(tokens, slots),
                vmem(2, *blocks, slots), vmem(*blocks, slots),
                vmem(3, 2, 256, slots), vmem(3, 2, 256, slots),
                vmem(3, 2, 6, 8, PAD, LANES), vmem(3, 2, 6, 8, PAD, LANES),
                vmem32(3, 2, 8, PAD, 256), vmem32(3, 2, 8, PAD, 256),
                vmem(3, 2, 3, 4, PAD, LANES), vmem(3, 2, 3, 4, PAD, LANES),
                vmem(3, 2, 3, PAD, LANES), vmem(3, 2, 3, PAD, LANES),
                pltpu.SemaphoreType.DMA((8,)),
                pltpu.SemaphoreType.DMA((N_MSG,)),
                pltpu.SemaphoreType.DMA((N_MSG,)),
            ],
            compiler_params=pltpu.CompilerParams(collective_id=0, has_side_effects=True, vmem_limit_bytes=VMEM_LIMIT),
        )(live_count, slot_token.reshape(1, slots), slot_prob.reshape(1, slots), expert_act.T, grad_out.T)
        return gradient * scaling

    both = ("dp", "tensor")
    return jax.shard_map(
        step,
        mesh=mesh,
        in_specs=(P(both, None), P(both, None), P(both), P(both), P(both)),
        out_specs=P("dp", "tensor"),
        check_vma=False,
    )
```

time: 46.6 us -> 40.6 us (0.87)
  Pallas kernels: 44.1 us -> 37.7 us
  other arithmetic: 0 us -> 0.67 us
    pallas_call x1, Pallas kernels: 44.1 us -> 37.7 us  [step(): pl.pallas_call(kernel, out_shape=jax.ShapeDtypeStruct((ROWS, HALF), F32),...]
    mul x0 -> x1, other arithmetic: none -> 0.67 us  [step(): return gradient * scaling]
    unnamed x1 -> x4, local copies, waits for them, and re-layouts: 1.58 us -> 1.36 us
where the time goes in v2:
time: 40.6 us; the launch traced here: 40.4 us
  Pallas kernels  37.7 us (93%)
  local copies, waits for them, and re-layouts  1.36 us (3%)
  other arithmetic  0.67 us (2%)
  between operations  0.67 us (2%)
    pallas_call x1, Pallas kernels, step(): pl.pallas_call(kernel, out_shape=jax.ShapeDtypeStruct((ROWS, HALF), F32),...  37.7 us
    unnamed x4, local copies, waits for them, and re-layouts  1.36 us

profile of v2, /device:TPU:0, one launch (start us, length us, event | category | flops | bytes accessed | tf_op | source)
XLA Modules:
  0.0 40.4 jit_solution(5878431775348571147)
XLA Ops:
  0.7 0.0 copy-start
  0.7 0.7 %copy-done = s32[512]{0:T(512)S(1)} copy-done((s32[512]{0:T(512)S(1)}, s32[512]{0:T(512)}, u32[]{:S(2)}) %copy-start) | copy-done | bytes 2072
  1.3 0.0 copy-start.1
  1.3 0.7 %copy-done.1 = f32[512]{0:T(512)S(1)} copy-done((f32[512]{0:T(512)S(1)}, f32[512]{0:T(512)}, u32[]{:S(2)}) %copy-start.1) | copy-done | bytes 2072
  2.0 37.7 %shard_map.55 = f32[45,720]{1,0:T(8,128)S(1)} custom-call(s32[1]{0:T(128)S(6)} %copy.6.live_ref, s32[1,512]{1,0:T(1,128)S(1)} %bitcast.4, f32[1,512]{1,0:T(1,128)S(1)} %bitcast.5, bf16[2880,512]{1,0:T(8,128)(2,1)} %bitcast.6, bf16[1440,1024]{1,0:T(8,128)(2,1)} %bitcast.7), custom_call_target="tpu_custom_call" | custom-call | tf_op jit(solution)/shard_map/pallas_call | solution.py:261
  39.7 0.7 %broadcast_multiply_fusion = f32[45,720]{1,0:T(8,128)} fusion(f32[45,720]{1,0:T(8,128)S(1)} %shard_map.55), kind=kLoop, calls=%fused_computation | loop fusion | flops 32400 | bytes 259200 | tf_op jit(solution)/shard_map/mul | solution.py:284
Async XLA Ops:
  0.7 0.7 %copy-start = (s32[512]{0:T(512)S(1)}, s32[512]{0:T(512)}, u32[]{:S(2)}) copy-start(s32[512]{0:T(512)} %param.7) | copy-start | bytes 6148
  1.3 0.7 %copy-start.1 = (f32[512]{0:T(512)S(1)}, f32[512]{0:T(512)}, u32[]{:S(2)}) copy-start(f32[512]{0:T(512)} %param.8) | copy-start | bytes 6148

commit v3 on v2

v3 whole, which is shorter than its diff:
```python
import math

import jax
import jax.numpy as jnp
from jax import lax
from jax.experimental import pallas as pl
from jax.experimental.pallas import tpu as pltpu
from jax.sharding import PartitionSpec as P

MESH = pl.DeviceIdType.MESH
F32, BF16 = jnp.float32, jnp.bfloat16
ROWS, PAD = 45, 48
WIDTHS = (256, 256, 208)
STARTS = (0, 256, 512)
HALF = 720
VMEM_LIMIT = 60 * 1024 * 1024
LANES = 128
A_IN, W_IN, FAR, NEAR, RELAY, SECOND, THIRD, N_IN = 0, 1, 4, 7, 10, 16, 22, 28
A_OUT, W_OUT, FAR_OUT, NEAR_OUT, RELAY_OUT, SECOND_OUT, THIRD_OUT, N_OUT = 0, 1, 2, 3, 4, 5, 6, 7


def nt(left, right):
    return lax.dot_general(left, right, (((1,), (1,)), ((), ())), preferred_element_type=F32)


def kernel(
    live_ref, tok_hbm, prob_hbm, a_hbm, g_hbm, out_ref,
    tok_ref, prob_ref, a_v, g_v, hot, ap, ao, wp, wo, sf, rf, sn, rn, sr, rr, keep, acc, s2, r2, s3, r3,
    load_sem, send_sem, recv_sem,
):
    dp, x_hi = lax.axis_index("dp"), lax.axis_index("tensor")
    core = lax.rem(dp, 2)
    x_lo = lax.rem(lax.div(dp, 2), 2)
    z = lax.rem(lax.div(dp, 4), 4)
    y = lax.div(dp, 16)
    x = x_hi * 2 + x_lo

    def at(cx, cy, cz, cc):
        return (((cy * 4 + cz) * 2 + lax.rem(cx, 2)) * 2 + cc, lax.div(cx, 2))

    def moved(dim, by):
        place = {"x": x, "y": y, "z": z}
        place[dim] = lax.rem(place[dim] + by, 4)
        return at(place["x"], place["y"], place["z"], core)

    partner = at(x, y, z, 1 - core)
    here = {"x": x, "y": y, "z": z}
    orders = ("yzx", "zxy", "xyz")

    chunk = a_v.shape[0] // 4
    loads = [(a_hbm.at[pl.ds(i * chunk, chunk)], a_v.at[pl.ds(i * chunk, chunk)]) for i in range(4)]
    loads += [(tok_hbm, tok_ref), (prob_hbm, prob_ref)]
    loads += [(g_hbm.at[pl.ds(i * HALF, HALF)], g_v.at[pl.ds(i * HALF, HALF)]) for i in range(2)]
    loads = [pltpu.make_async_copy(src, dst, load_sem.at[i]) for i, (src, dst) in enumerate(loads)]
    for load in loads:
        load.start()

    barrier = pltpu.get_barrier_semaphore()
    peers = [partner] + [moved(d, by) for d in "xyz" for by in (1, 2, 3)]
    for peer in peers:
        pl.semaphore_signal(barrier, inc=1, device_id=peer, device_id_type=MESH)

    def copy(src, dst, out, into, device):
        return pltpu.make_async_remote_copy(
            src_ref=src, dst_ref=dst, send_sem=send_sem.at[out], recv_sem=recv_sem.at[into],
            device_id=device, device_id_type=MESH,
        )

    def send(src, dst, out, into, device):
        copy(src, dst, out, into, device).start()

    def arrived(src, dst, out, into):
        copy(src, dst, out, into, partner).wait_recv()

    tokens, slots = hot.shape
    zeros = jnp.zeros((PAD - ROWS, slots), F32)

    def padded(quarter):
        for parity in range(2):
            for q in range(8):
                first = ROWS * (16 * quarter + 2 * q + parity)
                base = first // 8 * 8
                stop = min(base + 56, (quarter + 1) * chunk)
                block = a_v[base:stop, :].astype(F32)[first - base : first - base + ROWS]
                block = jnp.concatenate([block, zeros], axis=0)
                ap[parity, quarter, q // 2, q % 2] = block.astype(BF16)

    for quarter in range(4):
        with jax.named_scope(f"pad{quarter}"):
            loads[quarter].wait()
            padded(quarter)
        if quarter == 0:
            with jax.named_scope("barrier"):
                pl.semaphore_wait(barrier, len(peers))
        send(ap.at[1 - core, quarter], ao.at[quarter], A_OUT, A_IN, partner)

    with jax.named_scope("hot"):
        loads[4].wait()
        loads[5].wait()
        for start in range(0, tokens, 256):
            rows = lax.broadcasted_iota(jnp.int32, (256, slots), 0) + start
            hot[start : start + 256, :] = (rows == tok_ref[...]).astype(F32).astype(BF16)
        position = lax.broadcasted_iota(jnp.int32, (1, slots), 1)
        weighting = jnp.where(position < live_ref[0], prob_ref[...], jnp.zeros((1, slots), F32))

    with jax.named_scope("weighted"):
        loads[6].wait()
        loads[7].wait()
        for k in range(3):
            width = WIDTHS[k]
            for half in range(2):
                first = half * HALF + STARTS[k]
                picked = jnp.dot(g_v[first : first + width, :], hot[...], preferred_element_type=F32)
                wp[k, half, :width, :] = (picked * weighting).astype(BF16)
                if width < 256:
                    wp[k, half, width:, :] = jnp.zeros((256 - width, slots), BF16)
            send(wp.at[k], wo.at[k], W_OUT, W_IN + k, partner)

    with jax.named_scope("swap_a"):
        arrived(ap.at[0], ao, A_OUT, A_IN)

    def unit(k, place, half):
        if k == 0:
            own, other, right = ap[core, place], ao[place], (k, half)
        elif k == 1:
            own, other, right = ap[core, :, place], ao[:, place], (k, half)
        else:
            low = lax.rem(place, 2)
            own = ap[core, 2 * half : 2 * half + 2, :, low]
            other = ao[2 * half : 2 * half + 2, :, low]
            right = (k, lax.div(place, 2))
        own, other = own.reshape(8 * PAD, slots), other.reshape(8 * PAD, slots)
        return (nt(own, wp[right]) + nt(other, wo[right])).reshape(8, PAD, 256)

    def lanes(part):
        return slice(part * LANES, part * LANES + LANES)

    ends = []
    for k in range(3):
        dim = orders[k][0]
        far, up, down = [lax.rem(here[dim] + by, 4) for by in (2, 1, 3)]
        ends.append((far, up, down, (moved(dim, 1), moved(dim, 3))))
    for k, (far, _, _, sides) in enumerate(ends):
        with jax.named_scope(f"swap_w{k}"):
            arrived(wp.at[k], wo.at[k], W_OUT, W_IN + k)
        with jax.named_scope(f"m1_{k}"):
            for half in range(2):
                sf[k, half] = unit(k, far, half).astype(BF16)
            for half in range(2):
                send(sf.at[k, half], rf.at[k, half], FAR_OUT, FAR + k, sides[half])
    with jax.named_scope("m2"):
        for k, (_, up, down, sides) in enumerate(ends):
            sn[k, 0] = unit(k, up, 1).astype(BF16)
            sn[k, 1] = unit(k, down, 0).astype(BF16)
        for k, (_, _, _, sides) in enumerate(ends):
            for side in range(2):
                send(sn.at[k, side], rn.at[k, side], NEAR_OUT, NEAR + k, sides[side])
    with jax.named_scope("keep"):
        for k, (_, up, down, _) in enumerate(ends):
            keep[k, 0] = unit(k, up, 0)
            keep[k, 1] = unit(k, down, 1)
    with jax.named_scope("own"):
        for k in range(3):
            for half in range(2):
                acc[k, half] = unit(k, here[orders[k][0]], half)
    for part in range(2):
        cols = lanes(part)
        for k, (_, _, _, sides) in enumerate(ends):
            with jax.named_scope(f"m3_{part}{k}"):
                if part == 0:
                    arrived(sf.at[k], rf.at[k], FAR_OUT, FAR + k)
                for half in range(2):
                    sr[k, part, half] = (keep[k, half, :, :, cols] + rf[k, half, :, :, cols].astype(F32)).astype(BF16)
                for half in range(2):
                    send(sr.at[k, part, half], rr.at[k, part, half], RELAY_OUT, RELAY + 2 * k + part, sides[half])

    def stage_two(k, place, cols):
        if k == 0:
            return acc[0, :, pl.ds(place * 2, 2), :, cols].reshape(4, PAD, LANES)
        hi, lo = lax.div(place, 2), lax.rem(place, 2)
        if k == 1:
            return jnp.stack([acc[1, hi, 2 * cy + lo, :, cols] for cy in range(4)])
        return acc[2, hi, pl.ds(lo * 4, 4), :, cols]

    for k in range(3):
        with jax.named_scope(f"m2_wait_{k}"):
            arrived(sn.at[k], rn.at[k], NEAR_OUT, NEAR + k)
            for half in range(2):
                acc[k, half] = acc[k, half] + rn[k, 1 - half].astype(F32)
    for part in range(2):
        cols = lanes(part)
        for k in range(3):
            dim = orders[k][1]
            with jax.named_scope(f"m3_wait_{part}{k}"):
                arrived(sr.at[k, part], rr.at[k, part], RELAY_OUT, RELAY + 2 * k + part)
                for half in range(2):
                    acc[k, half, :, :, cols] = acc[k, half, :, :, cols] + rr[k, part, half].astype(F32)
            with jax.named_scope(f"s2_send_{part}{k}"):
                for i, by in enumerate((2, 1, 3)):
                    s2[k, part, i] = stage_two(k, lax.rem(here[dim] + by, 4), cols).astype(BF16)
                for i, by in enumerate((2, 1, 3)):
                    send(s2.at[k, part, i], r2.at[k, part, i], SECOND_OUT, SECOND + 2 * k + part, moved(dim, by))
    for part in range(2):
        cols = lanes(part)
        for k in range(3):
            dim = orders[k][2]
            with jax.named_scope(f"s2_wait_{part}{k}"):
                total = stage_two(k, here[orders[k][1]], cols)
                arrived(s2.at[k, part], r2.at[k, part], SECOND_OUT, SECOND + 2 * k + part)
                for i in range(3):
                    total = total + r2[k, part, i].astype(F32)
                keep[k, part, 0:4, :, :LANES] = total
            with jax.named_scope(f"s3_send_{part}{k}"):
                for i, by in enumerate((2, 1, 3)):
                    s3[k, part, i] = keep[k, part, lax.rem(here[dim] + by, 4), :, :LANES].astype(BF16)
                for i, by in enumerate((2, 1, 3)):
                    send(s3.at[k, part, i], r3.at[k, part, i], THIRD_OUT, THIRD + 2 * k + part, moved(dim, by))
    for part in range(2):
        for k in range(3):
            with jax.named_scope(f"s3_wait_{part}{k}"):
                total = keep[k, part, here[orders[k][2]], :, :LANES]
                arrived(s3.at[k, part], r3.at[k, part], THIRD_OUT, THIRD + 2 * k + part)
                for i in range(3):
                    total = total + r3[k, part, i].astype(F32)
                first = STARTS[k] + part * LANES
                last = min(first + LANES, STARTS[k] + WIDTHS[k])
                out_ref[:, first:last] = total[:ROWS, : last - first]
    with jax.named_scope("drain"):
        leaving = ((ap.at[0], ao), (wp, wo), (sf, rf), (sn, rn), (sr, rr), (s2, r2), (s3, r3))
        for out, (src, dst) in enumerate(leaving):
            copy(src, dst, out, 0, partner).wait_send()


def solution(mesh):
    devices = mesh.shape["dp"] * mesh.shape["tensor"]

    def step(expert_act, grad_out, slot_token, slot_prob, live_count):
        slots, hidden = expert_act.shape
        tokens, features = grad_out.shape
        scaling = 1.0 / math.sqrt(slots * devices)
        blocks = (4, 4, 2, PAD)
        vmem = lambda *shape: pltpu.VMEM(shape, BF16)
        vmem32 = lambda *shape: pltpu.VMEM(shape, F32)
        gradient = pl.pallas_call(
            kernel,
            out_shape=pltpu.VMEM((ROWS, HALF), F32),
            in_specs=[
                pl.BlockSpec(memory_space=pltpu.SMEM),
                *[pl.BlockSpec(memory_space=pltpu.HBM)] * 4,
            ],
            out_specs=pl.BlockSpec(memory_space=pltpu.VMEM),
            scratch_shapes=[
                pltpu.VMEM((1, slots), jnp.int32), vmem32(1, slots),
                vmem(hidden, slots), vmem(features, tokens), vmem(tokens, slots),
                vmem(2, *blocks, slots), vmem(*blocks, slots),
                vmem(3, 2, 256, slots), vmem(3, 2, 256, slots),
                vmem(3, 2, 8, PAD, 256), vmem(3, 2, 8, PAD, 256),
                vmem(3, 2, 8, PAD, 256), vmem(3, 2, 8, PAD, 256),
                vmem(3, 2, 2, 8, PAD, LANES), vmem(3, 2, 2, 8, PAD, LANES),
                vmem32(3, 2, 8, PAD, 256), vmem32(3, 2, 8, PAD, 256),
                vmem(3, 2, 3, 4, PAD, LANES), vmem(3, 2, 3, 4, PAD, LANES),
                vmem(3, 2, 3, PAD, LANES), vmem(3, 2, 3, PAD, LANES),
                pltpu.SemaphoreType.DMA((8,)),
                pltpu.SemaphoreType.DMA((N_OUT,)),
                pltpu.SemaphoreType.DMA((N_IN,)),
            ],
            compiler_params=pltpu.CompilerParams(collective_id=0, has_side_effects=True, vmem_limit_bytes=VMEM_LIMIT),
        )(live_count, slot_token.reshape(1, slots), slot_prob.reshape(1, slots), expert_act.T, grad_out.T)
        return gradient * scaling

    both = ("dp", "tensor")
    return jax.shard_map(
        step,
        mesh=mesh,
        in_specs=(P(both, None), P(both, None), P(both), P(both), P(both)),
        out_specs=P("dp", "tensor"),
        check_vma=False,
    )
```

time: 40.6 us -> 38.4 us (0.946)
  local copies, waits for them, and re-layouts: 1.36 us -> 0 us
  Pallas kernels: 37.7 us -> 36.6 us
    unnamed x4 -> x0, local copies, waits for them, and re-layouts: 1.36 us -> none
    pallas_call x1, Pallas kernels: 37.7 us -> 36.6 us  [step(): pl.pallas_call(kernel, out_shape=pltpu.VMEM((ROWS, HALF), F32), in_specs=...]
where the time goes in v3:
time: 38.4 us; the launch traced here: 38 us
  Pallas kernels  36.6 us (95%)
  other arithmetic  0.67 us (2%)
  between operations  0.66 us (2%)
    pallas_call x1, Pallas kernels, step(): pl.pallas_call(kernel, out_shape=pltpu.VMEM((ROWS, HALF), F32), in_specs=...  36.6 us

profile of v3, /device:TPU:0, one launch (start us, length us, event | category | flops | bytes accessed | tf_op | source)
XLA Modules:
  0.0 38.0 jit_solution(6880898661846321545)
XLA Ops:
  0.7 36.6 %shard_map.55 = f32[45,720]{1,0:T(8,128)S(1)} custom-call(s32[1]{0:T(128)S(6)} %copy.6.live_ref, s32[1,512]{1,0:T(1,128)} %bitcast.6, f32[1,512]{1,0:T(1,128)} %bitcast.7, bf16[2880,512]{1,0:T(8,128)(2,1)} %bitcast.4, bf16[1440,1024]{1,0:T(8,128)(2,1)} %bitcast.5), custom_call_target="tpu_custom_call" | custom-call | tf_op jit(solution)/shard_map/pallas_call | solution.py:244
  37.3 0.7 %broadcast_multiply_fusion = f32[45,720]{1,0:T(8,128)} fusion(f32[45,720]{1,0:T(8,128)S(1)} %shard_map.55), kind=kLoop, calls=%fused_computation | loop fusion | flops 32400 | bytes 259200 | tf_op jit(solution)/shard_map/mul | solution.py:269
